TPU v7x, 32 devices: a whole 2x2x4 slice. The times are simulated.
32 devices in a mesh: lat: 16 (over z, x, core), tm: 2 (over y).
Axes of the slice: x: 2, y: 2, z: 4, core: 2. Of those that a mesh axis runs over, the one named last changes fastest.
Arguments:
- fields: bfloat16 [512, 64, 1024], P('lat', 'tm'), may hold values from -16 to 16
Outputs:
- covariance: float32 [64, 64], P('tm')
All inputs are finite; a program needn't handle non-finite values.
Results may differ from a plain program's by a relative error of at most 0.0003.
Values may be sent and summed in bfloat16 or wider, within the bound.
A program may use at most 64 MiB of HBM per device.

v0:
```python
import math
import jax
import jax.numpy as jnp
from jax import lax
from jax.sharding import PartitionSpec as P

TRUNC = 341
MSLOT = 384
DSLOT = 384


def start_value(order, sine_lat):
    log_start = 0.5 * (
        math.log(0.5)
        + lax.lgamma(order + 1.5)
        - (0.5 * math.log(math.pi) - math.log(2.0))
        - lax.lgamma(order + 1.0)
    ) + order * jnp.log(sine_lat)
    taper = jnp.clip((log_start + 70.0) / 10.0, 0.0, 1.0)
    return jnp.exp(jnp.maximum(log_start, -80.0)) * taper


def step_factors(order, degree):
    top = jnp.sqrt((4.0 * degree * degree - 1.0) / (degree * degree - order * order))
    below = degree - 1.0
    back = jnp.sqrt(
        jnp.maximum(below * below - order * order, 0.0) / jnp.abs(4.0 * below * below - 1.0)
    )
    return (top, top * back)


def legendre_blocks(orders, cosine_lat, sine_lat):
    order_total = orders.shape[0]
    lat_total = cosine_lat.shape[0]
    block_total = 16
    block_length = DSLOT // block_total
    order_grid = orders[:, None, None]
    cosine_grid = cosine_lat[None, :, None]
    block_base = (jnp.arange(block_total) * block_length).astype(jnp.float32)[None, None, :]
    unit = jnp.ones((order_total, lat_total, block_total), jnp.float32)
    empty = jnp.zeros_like(unit)

    def compose(position, matrices):
        upper_left, upper_right, lower_left, lower_right = matrices
        top, mixed = step_factors(
            order_grid, order_grid + block_base + position.astype(jnp.float32)
        )
        diagonal_term = top * cosine_grid
        return (
            diagonal_term * upper_left - mixed * lower_left,
            diagonal_term * upper_right - mixed * lower_right,
            upper_left,
            upper_right,
        )

    upper_left, upper_right, lower_left, lower_right = lax.fori_loop(
        1, block_length + 1, compose, (unit, empty, empty, unit)
    )
    current = start_value(orders[:, None], sine_lat[None, :])
    previous = jnp.zeros_like(current)
    current_list = []
    previous_list = []
    for block in range(block_total):
        current_list.append(current)
        previous_list.append(previous)
        current, previous = (
            upper_left[:, :, block] * current + upper_right[:, :, block] * previous,
            lower_left[:, :, block] * current + lower_right[:, :, block] * previous,
        )
    current = jnp.stack(current_list, axis=-1)
    previous = jnp.stack(previous_list, axis=-1)
    outputs = []
    for position in range(1, block_length + 1):
        outputs.append(current)
        top, mixed = step_factors(order_grid, order_grid + block_base + float(position))
        current, previous = (top * cosine_grid * current - mixed * previous, current)
    values = jnp.stack(outputs, axis=-1)
    return values.reshape(order_total, lat_total, DSLOT)


def weighted_basis(orders, cosine_lat, sine_lat, weight):
    values = legendre_blocks(orders, cosine_lat, sine_lat)
    offsets = jnp.arange(DSLOT).astype(jnp.float32)
    keep = (orders[:, None] + offsets[None, :] <= TRUNC).astype(jnp.float32)
    factor = jnp.where(orders > 0, math.sqrt(2.0), 1.0)
    table = values * keep[:, None, :] * weight[None, :, None] * factor[:, None, None]
    return table.astype(jnp.bfloat16)


def local(fields):
    row_count, month_count, lon_count = fields.shape
    lat_devices = lax.axis_size("lat")
    slots_dev = MSLOT // lat_devices
    lat_index = lax.axis_index("lat")
    column = jnp.arange(2 * MSLOT)
    group = column // (2 * slots_dev)
    inner = column % (2 * slots_dev) // 2
    part_index = column % 2
    own_inner = jnp.arange(slots_dev)
    wave_order = group * slots_dev + inner
    own_order = lat_index * slots_dev + own_inner
    longitude = jnp.arange(lon_count)
    phase = (
        2.0
        * math.pi
        * (wave_order[:, None] * longitude[None, :] % lon_count).astype(jnp.float32)
        / lon_count
    )
    active = (wave_order <= TRUNC).astype(jnp.float32)[:, None]
    transform = (
        jnp.where(part_index[:, None] == 0, jnp.cos(phase), -jnp.sin(phase))
        * active
        / math.sqrt(lon_count)
    )
    transform = transform.astype(jnp.bfloat16)
    flat_fields = fields.reshape(row_count * month_count, lon_count)
    fourier = lax.dot_general(
        transform, flat_fields, (((1,), (1,)), ((), ())), preferred_element_type=jnp.float32
    )
    fourier = fourier.astype(jnp.bfloat16).reshape(2 * MSLOT, row_count, month_count)
    moved = lax.all_to_all(fourier, "lat", split_axis=0, concat_axis=1, tiled=True)
    lat_count = moved.shape[1]
    theta = math.pi * (jnp.arange(lat_count).astype(jnp.float32) + 0.5) / lat_count
    cosine_lat = jnp.cos(theta)
    sine_lat = jnp.sin(theta)
    weight = math.pi * sine_lat / lat_count
    basis = weighted_basis(own_order.astype(jnp.float32), cosine_lat, sine_lat, weight)
    moved_data = moved.reshape(slots_dev, 2, lat_count, month_count)
    coefficients = jnp.einsum(
        "srjt,sjd->tsrd", moved_data, basis, preferred_element_type=jnp.float32
    )
    coefficients = coefficients.astype(jnp.bfloat16).reshape(month_count, -1)
    tm_devices = lax.axis_size("tm")
    total_months = month_count * tm_devices
    columns = lax.all_to_all(coefficients, "tm", split_axis=1, concat_axis=0, tiled=True)
    partial_gram = lax.psum_scatter(
        lax.dot_general(
            columns, columns, (((1,), (1,)), ((), ())), preferred_element_type=jnp.float32
        ),
        "tm",
        scatter_dimension=0,
        tiled=True,
    )
    gram = lax.psum(partial_gram, "lat")
    own_block = lax.dynamic_slice_in_dim(gram, lax.axis_index("tm") * month_count, month_count, 1)
    trace_total = lax.psum(jnp.sum(jnp.diagonal(own_block)), "tm")
    return total_months * gram / (trace_total + 1e-06)


def solution(mesh):
    placed = (P("lat", "tm", None),)
    return jax.shard_map(
        local, mesh=mesh, in_specs=placed, out_specs=P("tm", None), check_vma=False
    )
```

profile of v0, /device:TPU:0, one launch (start us, length us, event | category | flops | bytes accessed | tf_op | source)
XLA Modules:
  0.0 353.8 jit_solution(13318265986543368269)
XLA Ops:
  8.1 16.4 %convolution_convert_fusion = bf16[768,1024]{1,0:T(8,128)(2,1)} fusion(bf16[1024,1024]{1,0:T(8,128)(2,1)S(1)} %bitcast.84, f32[768]{0:T(1024)S(1)} %get-tuple-element.432, s32[768]{0:T(1024)S(1)} %fusion.324, pred[768]{0:T(1024)(128)(4,1)S(1)} %get-tuple-element.431), kind=kOutput, calls=%fused_computation.41 | convolution fusion | flops 1626341376 | bytes 3676928 | tf_op jit(solution)/shard_map/dot_general | solution.py:117
  26.2 9.2 %copy.128 = bf16[768,32,32]{2,1,0:T(8,128)(2,1)} copy(bf16[768,32,32]{0,2,1:T(8,128)(2,1)S(1)} %bitcast.90) | data formatting | bytes 3145728 | tf_op jit(solution)/shard_map/reshape | solution.py:120
  35.4 9.3 %reshape.8823 = bf16[16,2,24576]{2,1,0:T(2,128)(2,1)} reshape(bf16[768,32,32]{2,1,0:T(8,128)(2,1)} %copy.128) | data formatting | bytes 3145728
  44.7 7.4 %all-to-all-start = ((bf16[16,2,24576]{2,1,0:T(2,128)(2,1)}), bf16[16,2,24576]{2,1,0:T(2,128)(2,1)}, u32[]{:S(2)}, u32[]{:S(2)}) async-start(bf16[16,2,24576]{2,1,0:T(2,128)(2,1)} %reshape.8823), calls=%async_computation | async-start | bytes 3145728 | tf_op jit(solution)/shard_map/all_to_all | solution.py:121
  53.3 71.6 %while.25 = (s32[]{:T(128)}, f32[24,512,16]{1,2,0:T(8,128)S(1)}, f32[24,512,16]{1,2,0:T(8,128)}, f32[24,512,16]{1,2,0:T(8,128)S(1)}, f32[24,512,16]{1,2,0:T(8,128)S(1)}, /*index=5*/s32[]{:T(128)}, s32[]{:T(128)}, s32[]{:T(128)}) while((s32[]{:T(128)}, f32[24,512,16]{1,2,0:T(8,128)S(1)}, ...), condition=%wide.region_1.2_spmd.clone.clone.clone, body=%wide.region_0.1_spmd.clone.clone.clone.sunk | while | flops 1778076 | bytes 6308475 | solution.py:56
  58.6 2.7 fusion.362
  61.6 2.7 fusion.362
  64.6 2.7 fusion.362
  67.6 2.7 fusion.362
  70.7 2.7 fusion.362
  73.7 2.7 fusion.362
  79.8 2.7 fusion.362
  125.6 6.1 %add_bitcast_fusion = (f32[24,512,1,1]{1,2,3,0:T(1,128)S(1)}, f32[24,512,1]{1,2,0:T(1,128)S(1)}, f32[24,512,1]{1,2,0:T(1,128)S(1)}, f32[24,512,1]{1,2,0:T(1,128)...) fusion(f32[24,512,16]{1,2,0:T(8,128)S(1)} %get-tuple-element.24, ...), kind=kLoop, calls=%fused_computation.123 | loop fusion | flops 1155072 | bytes 4278464 | tf_op jit(solution)/shard_map/stack | solution.py:71
  152.9 3.0 stack.164
  186.8 17.4 %copy.126 = f32[24,512,16,24]{1,3,2,0:T(8,128)S(1)} copy(f32[24,512,16,24]{1,2,3,0:T(8,128)} %subtract_dynamic-update-slice_fusion) | data formatting | bytes 37748736 | tf_op jit(solution)/shard_map/stack | solution.py:77
  204.4 6.3 %fusion.20 = bf16[24,512,384]{1,2,0:T(8,128)(2,1)} fusion(f32[24,512,16,24]{1,3,2,0:T(8,128)S(1)} %copy.126, f32[24]{0:T(128)S(1)} %copy-done.23, f32[512]{0:T(512)S(1)} %fusion.337, f32[24,384]{1,0:T(8,128)S(1)} %fusion.38), kind=kLoop, calls=%fused_computation.30 | loop fusion | flops 18874368 | bytes 28350560 | tf_op jit(solution)/shard_map/convert_element_type | solution.py:87
  210.6 7.9 %reshape.8824 = bf16[768,32,32]{2,1,0:T(8,128)(2,1)} reshape(bf16[16,2,24576]{2,1,0:T(2,128)(2,1)} %all-to-all-done) | data formatting | bytes 3145728
  218.5 9.5 %copy.129 = bf16[16,48,32,32]{2,0,3,1:T(8,128)(2,1)} copy(bf16[16,48,32,32]{3,2,1,0:T(8,128)(2,1)} %bitcast.85) | data formatting | bytes 3145728 | tf_op jit(solution)/shard_map/all_to_all | solution.py:121
  228.0 9.3 %reshape.8814 = bf16[24,2,512,32]{2,3,1,0:T(8,128)(2,1)} reshape(bf16[48,16,32,32]{2,1,3,0:T(8,128)(2,1)} %bitcast.86) | data formatting | bytes 3145728 | tf_op jit(solution)/shard_map/reshape | solution.py:128
  237.3 7.0 %fusion.352 = f32[24,384,64]{1,2,0:S(1)} fusion(bf16[24,512,384]{1,2,0:T(8,128)(2,1)} %fusion.20, bf16[24,512,64]{1,2,0:T(8,128)(2,1)} %bitcast.89), kind=kOutput, calls=%fused_computation.517 | convolution fusion | flops 603979776 | bytes 13369344
  248.6 18.3 %all_to_all.34 = bf16[32,2,9216]{2,0,1:T(8,128)(2,1)S(1)} all-to-all(bf16[32,2,9216]{2,0,1:T(8,128)(2,1)S(1)} %copy.132), channel_id=1, replica_groups=mesh['lat'=16,'tm'=2] {'tm'}, dimensions={1} | all-to-all | bytes 2359296 | tf_op jit(solution)/shard_map/all_to_all | solution.py:135
  267.9 10.2 %reduce-scatter.2.cloned.1.call-done = f32[32,64]{1,0:T(8,128)} async-done(((f32[64,64]{1,0:T(8,128)}), f32[32,64]{1,0:T(8,128)}) %reduce-scatter.2.cloned.1.call-update) | async-done | bytes 8208 | tf_op jit(solution)/shard_map/reduce_scatter | solution.py:136
  278.1 60.6 %psum.14 = f32[32,64]{1,0:T(8,128)S(1)} all-reduce(f32[32,64]{1,0:T(8,128)} %reduce-scatter.2.cloned.1.call-done), channel_id=1, replica_groups=mesh['lat'=16,'tm'=2] {'lat'}, use_global_device_ids=true, to_apply=%region_3.4 | all-reduce | flops 2048 | bytes 16384 | tf_op jit(solution)/shard_map/psum | solution.py:144
  340.1 5.5 %psum.15 = f32[]{:T(128)} all-reduce(f32[]{:T(128)} %reduce_sum.9), channel_id=1, replica_groups=mesh['lat'=16,'tm'=2] {'tm'}, use_global_device_ids=true, to_apply=%region_5.6 | all-reduce | flops 1 | bytes 8 | tf_op jit(solution)/shard_map/psum | solution.py:146
  (338 shorter events, 116.8 us)
Async XLA Ops:
  44.7 165.9 %all-to-all-start = ((bf16[16,2,24576]{2,1,0:T(2,128)(2,1)}), bf16[16,2,24576]{2,1,0:T(2,128)(2,1)}, u32[]{:S(2)}, u32[]{:S(2)}) async-start(bf16[16,2,24576]{2,1,0:T(2,128)(2,1)} %reshape.8823), calls=%async_computation | async-start | bytes 3145728 | tf_op jit(solution)/shard_map/all_to_all | solution.py:121
  52.2 226.0 %reduce-scatter.2.cloned.1.call-start = ((), (), s32[]{:S(2)}) async-start(), calls=%async_computation.3 | async-start | bytes 49152 | tf_op jit(solution)/shard_map/reduce_scatter | solution.py:136
  52.4 82.7 %copy-start.21 = (f32[24]{0:T(128)}, f32[24]{0:T(128)S(1)}, u32[]{:S(2)}) copy-start(f32[24]{0:T(128)S(1)} %add_convert_fusion) | copy-start | bytes 292
  152.8 13.9 %copy-start.13 = (f32[24,16]{1,0:T(8,128)S(1)}, f32[24,16]{1,0:T(8,128)}, u32[]{:S(2)}) copy-start(f32[24,16]{1,0:T(8,128)} %copy.93) | copy-start | bytes 4612
  152.8 17.5 %copy-start.12 = (f32[24,16]{1,0:T(8,128)S(1)}, f32[24,16]{1,0:T(8,128)}, u32[]{:S(2)}) copy-start(f32[24,16]{1,0:T(8,128)} %copy.100) | copy-start | bytes 4612
  152.8 17.5 %copy-start.14 = (f32[24,16]{1,0:T(8,128)S(1)}, f32[24,16]{1,0:T(8,128)}, u32[]{:S(2)}) copy-start(f32[24,16]{1,0:T(8,128)} %copy.99) | copy-start | bytes 4612
  152.8 18.8 %copy-start.9 = (f32[24,16]{1,0:T(8,128)S(1)}, f32[24,16]{1,0:T(8,128)}, u32[]{:S(2)}) copy-start(f32[24,16]{1,0:T(8,128)} %copy.101) | copy-start | bytes 4612
  152.8 18.8 %copy-start.11 = (f32[24,16]{1,0:T(8,128)S(1)}, f32[24,16]{1,0:T(8,128)}, u32[]{:S(2)}) copy-start(f32[24,16]{1,0:T(8,128)} %copy.102) | copy-start | bytes 4612
  157.1 18.2 %copy-start.8 = (f32[24,16]{1,0:T(8,128)S(1)}, f32[24,16]{1,0:T(8,128)}, u32[]{:S(2)}) copy-start(f32[24,16]{1,0:T(8,128)} %copy.107) | copy-start | bytes 4612
  157.1 18.2 %copy-start.10 = (f32[24,16]{1,0:T(8,128)S(1)}, f32[24,16]{1,0:T(8,128)}, u32[]{:S(2)}) copy-start(f32[24,16]{1,0:T(8,128)} %copy.108) | copy-start | bytes 4612
  158.3 18.3 %copy-start.6 = (f32[24,16]{1,0:T(8,128)S(1)}, f32[24,16]{1,0:T(8,128)}, u32[]{:S(2)}) copy-start(f32[24,16]{1,0:T(8,128)} %copy.109) | copy-start | bytes 4612
  158.3 18.3 %copy-start.7 = (f32[24,16]{1,0:T(8,128)S(1)}, f32[24,16]{1,0:T(8,128)}, u32[]{:S(2)}) copy-start(f32[24,16]{1,0:T(8,128)} %copy.110) | copy-start | bytes 4612
  162.3 16.7 %copy-start.4 = (f32[24,16]{1,0:T(8,128)S(1)}, f32[24,16]{1,0:T(8,128)}, u32[]{:S(2)}) copy-start(f32[24,16]{1,0:T(8,128)} %copy.113) | copy-start | bytes 4612
  162.3 16.7 %copy-start.5 = (f32[24,16]{1,0:T(8,128)S(1)}, f32[24,16]{1,0:T(8,128)}, u32[]{:S(2)}) copy-start(f32[24,16]{1,0:T(8,128)} %copy.114) | copy-start | bytes 4612
  164.6 15.6 %copy-start.2 = (f32[24,16]{1,0:T(8,128)S(1)}, f32[24,16]{1,0:T(8,128)}, u32[]{:S(2)}) copy-start(f32[24,16]{1,0:T(8,128)} %copy.115) | copy-start | bytes 4612
  164.6 15.7 %copy-start.3 = (f32[24,16]{1,0:T(8,128)S(1)}, f32[24,16]{1,0:T(8,128)}, u32[]{:S(2)}) copy-start(f32[24,16]{1,0:T(8,128)} %copy.116) | copy-start | bytes 4612
  168.0 14.5 %copy-start.20 = (f32[24,16]{0,1:T(8,128)S(1)}, f32[24,16]{0,1:T(8,128)}, u32[]{:S(2)}) copy-start(f32[24,16]{0,1:T(8,128)} %get-tuple-element.404) | copy-start | bytes 4612
  168.0 14.6 %copy-start.19 = (f32[24,16]{0,1:T(8,128)S(1)}, f32[24,16]{0,1:T(8,128)}, u32[]{:S(2)}) copy-start(f32[24,16]{0,1:T(8,128)} %get-tuple-element.408) | copy-start | bytes 4612
  168.0 14.7 %copy-start.18 = (f32[24,16]{0,1:T(8,128)S(1)}, f32[24,16]{0,1:T(8,128)}, u32[]{:S(2)}) copy-start(f32[24,16]{0,1:T(8,128)} %get-tuple-element.405) | copy-start | bytes 4612
  168.0 14.7 %copy-start.17 = (f32[24,16]{0,1:T(8,128)S(1)}, f32[24,16]{0,1:T(8,128)}, u32[]{:S(2)}) copy-start(f32[24,16]{0,1:T(8,128)} %get-tuple-element.407) | copy-start | bytes 4612
  168.0 14.8 %copy-start.16 = (f32[24,16]{0,1:T(8,128)S(1)}, f32[24,16]{0,1:T(8,128)}, u32[]{:S(2)}) copy-start(f32[24,16]{0,1:T(8,128)} %get-tuple-element.383) | copy-start | bytes 4612
  186.8 17.5 %copy-start.22 = (f32[24]{0:T(128)S(1)}, f32[24]{0:T(128)}, u32[]{:S(2)}) copy-start(f32[24]{0:T(128)} %copy-done.21) | copy-start | bytes 292
  186.8 17.5 %copy-start.23 = (f32[24]{0:T(128)S(1)}, f32[24]{0:T(128)}, u32[]{:S(2)}) copy-start(f32[24]{0:T(128)} %get-tuple-element.429) | copy-start | bytes 292
  218.5 128.4 %copy-start.1 = (bf16[32,32,1024]{2,1,0:T(8,128)(2,1)S(1)}, bf16[32,32,1024]{2,1,0:T(8,128)(2,1)}, u32[]{:S(2)}) copy-start(bf16[32,32,1024]{2,1,0:T(8,128)(2,1)} %param.3) | copy-start | bytes 6291460
  (2 other events, 15.5 us)
Sparse Core Ops, SparseCore 0:
  268.0 10.0 reduce-scatter.1
where the time goes:
time: 356 us; the launch traced here: 354 us
  other arithmetic  115 us (32%)
  local copies, waits for them, and re-layouts  96.8 us (27%)
  blocking collectives  84.4 us (24%)
  matrix products  24.4 us (7%)
  between operations  14.4 us (4%)
  waiting for transfers between devices  10.2 us (3%)
  starting transfers between devices  7.65 us (2%)
    sub x24, other arithmetic, compose(): diagonal_term * upper_right - mixed * lower_right  63.1 us
    psum x1, blocking collectives, local(): gram = lax.psum(partial_gram, 'lat')  60.6 us
    unnamed x24, other arithmetic  29 us
    unnamed x51, local copies, waits for them, and re-layouts  19.8 us
    all_to_all x1, blocking collectives, local(): lax.all_to_all(coefficients, 'tm', split_axis=1, concat_axis=0, tiled=True)  18.3 us
    another operation x1, local copies, waits for them, and re-layouts, legendre_blocks(): values = jnp.stack(outputs, axis=-1)  17.4 us
    dot_general x1, matrix products, local(): lax.dot_general(transform, flat_fields, (((1,), (1,)), ((), ())), preferr...  16.4 us
    reduce_scatter x1, waiting for transfers between devices, local(): lax.psum_scatter(lax.dot_general(columns, columns, (((1,), (1,)), ((), ()...  10.2 us
  transfers between devices with their start and end apart: 2, of which 1 were waited for; matrix products, arithmetic and copies ran while one was open for 45% of the time, Pallas kernels for 0%

commit v1 on v0

--- a/solution.py
+++ b/solution.py
@@ -141,7 +141,7 @@
         scatter_dimension=0,
         tiled=True,
     )
-    gram = lax.psum(partial_gram, "lat")
+    gram = jnp.sum(lax.all_gather(partial_gram, "lat"), axis=0)
     own_block = lax.dynamic_slice_in_dim(gram, lax.axis_index("tm") * month_count, month_count, 1)
     trace_total = lax.psum(jnp.sum(jnp.diagonal(own_block)), "tm")
     return total_months * gram / (trace_total + 1e-06)

time: 356 us -> 280 us (0.79)
  other arithmetic: 115 us -> 66.3 us
  blocking collectives: 84.4 us -> 46.1 us
  local copies, waits for them, and re-layouts: 96.8 us -> 108 us
    psum x1 -> x0, blocking collectives: 60.6 us -> none  [local(): gram = lax.psum(partial_gram, 'lat')]
    sub x24, other arithmetic: 63.1 us -> 15.2 us  [compose(): diagonal_term * upper_right - mixed * lower_right]
    all_gather x0 -> x1, blocking collectives: none -> 22.3 us  [local(): gram = jnp.sum(lax.all_gather(partial_gram, 'lat'), axis=0)]
    unnamed x51 -> x85, local copies, waits for them, and re-layouts: 19.8 us -> 20.4 us
  transfers between devices with their start and end apart: 2 -> 2, of which waited for: 1 -> 1; matrix products, arithmetic and copies ran while one was open for 45% -> 41% of each run, Pallas kernels for 0% -> 0%
where the time goes in v1:
time: 280 us; the launch traced here: 278 us
  local copies, waits for them, and re-layouts  108 us (39%)
  other arithmetic  66.3 us (24%)
  blocking collectives  46.1 us (16%)
  matrix products  24.5 us (9%)
  between operations  14.5 us (5%)
  waiting for transfers between devices  10.2 us (4%)
  starting transfers between devices  7.65 us (3%)
    unnamed x24, other arithmetic  30.4 us
    all_gather x1, blocking collectives, local(): gram = jnp.sum(lax.all_gather(partial_gram, 'lat'), axis=0)  22.3 us
    unnamed x85, local copies, waits for them, and re-layouts  20.4 us
    all_to_all x1, blocking collectives, local(): lax.all_to_all(coefficients, 'tm', split_axis=1, concat_axis=0, tiled=True)  18.3 us
    another operation x1, local copies, waits for them, and re-layouts, legendre_blocks(): values = jnp.stack(outputs, axis=-1)  17.4 us
    dot_general x1, matrix products, local(): lax.dot_general(transform, flat_fields, (((1,), (1,)), ((), ())), preferr...  16.4 us
    sub x24, other arithmetic, compose(): diagonal_term * upper_right - mixed * lower_right  15.2 us
    mul x47, local copies, waits for them, and re-layouts, step_factors(): return (top, top * back)  12.3 us
  transfers between devices with their start and end apart: 2, of which 1 were waited for; matrix products, arithmetic and copies ran while one was open for 41% of the time, Pallas kernels for 0%

profile of v1, /device:TPU:0, one launch (start us, length us, event | category | flops | bytes accessed | tf_op | source)
XLA Modules:
  0.0 278.3 jit_solution(15512611404865712756)
XLA Ops:
  8.1 16.4 %convolution_convert_fusion = bf16[768,1024]{1,0:T(8,128)(2,1)} fusion(bf16[1024,1024]{1,0:T(8,128)(2,1)S(1)} %bitcast.85, f32[768]{0:T(1024)S(1)} %get-tuple-element.432, s32[768]{0:T(1024)S(1)} %fusion.324, pred[768]{0:T(1024)(128)(4,1)S(1)} %get-tuple-element.431), kind=kOutput, calls=%fused_computation.41 | convolution fusion | flops 1626341376 | bytes 3676928 | tf_op jit(solution)/shard_map/dot_general | solution.py:117
  26.2 9.2 %copy.128 = bf16[768,32,32]{2,1,0:T(8,128)(2,1)} copy(bf16[768,32,32]{0,2,1:T(8,128)(2,1)S(1)} %bitcast.91) | data formatting | bytes 3145728 | tf_op jit(solution)/shard_map/reshape | solution.py:120
  35.4 9.3 %reshape.8824 = bf16[16,2,24576]{2,1,0:T(2,128)(2,1)} reshape(bf16[768,32,32]{2,1,0:T(8,128)(2,1)} %copy.128) | data formatting | bytes 3145728
  44.8 7.4 %all-to-all-start = ((bf16[16,2,24576]{2,1,0:T(2,128)(2,1)}), bf16[16,2,24576]{2,1,0:T(2,128)(2,1)}, u32[]{:S(2)}, u32[]{:S(2)}) async-start(bf16[16,2,24576]{2,1,0:T(2,128)(2,1)} %reshape.8824), calls=%async_computation | async-start | bytes 3145728 | tf_op jit(solution)/shard_map/all_to_all | solution.py:121
  53.3 24.5 %while.25 = (s32[]{:T(128)}, f32[24,512,16]{1,2,0:T(8,128)S(1)}, f32[24,512,16]{1,2,0:T(8,128)S(1)}, f32[24,512,16]{1,2,0:T(8,128)S(1)}, f32[24,512,16]{1,2,0:T(8,128)S(1)}, /*index=5*/s32[]{:T(128)}, s32[]{:T(128)}, s32[]{:T(128)}) while((s32[]{:T(128)}, f32[24,512,16]{1,2,0:T(8,128)S(1)}, ...), condition=%wide.region_1.2_spmd.clone.clone.clone, body=%wide.region_0.1_spmd.clone.clone.clone.sunk | while | flops 1778076 | bytes 6308475 | solution.py:56
  78.7 4.1 %add_bitcast_fusion = (f32[24,512,1,1]{1,2,3,0:T(1,128)}, f32[24,512,1]{1,2,0:T(1,128)S(1)}, f32[24,512,1]{1,2,0:T(1,128)S(1)}, f32[24,512,1]{1,2,0:T(1,128)}, f...) fusion(f32[24,512,16]{1,2,0:T(8,128)S(1)} %get-tuple-element.24, ...), kind=kLoop, calls=%fused_computation.123 | loop fusion | flops 1155072 | bytes 4278464 | tf_op jit(solution)/shard_map/stack | solution.py:71
  83.4 2.1 stack.130
  107.5 2.1 stack.148
  109.8 3.2 %stack.164 = f32[24,512,16,1]{1,2,3,0:T(8,128)S(1)} concatenate(f32[24,512,1,1]{1,2,3,0:T(1,128)S(1)} %stack_broadcast_in_dim.3, f32[24,512,1,1]{1,2,3,0:T(1,128)} %bitcast.122, f32[24,512,1,1]{1,2,3,0:T(1,128)} %bitcast.121, f32[24,512,1,1]{1,2,3,0:T(1,128)} %bitcast.120, f32[24,512,1,1]{1,2,3,0:T(1,128)} %bitcast.119, f32[24,512,1,1]{1,2,3,0:T(1,128)} %bitcast.118, ...), dimensions={2} | concatenate | bytes 1572864 | tf_op jit(solution)/shard_map/stack | solution.py:71
  116.6 2.1 constant_dynamic-update-slice_fusion.15
  120.6 2.0 constant_dynamic-update-slice_fusion.13
  122.6 2.1 constant_dynamic-update-slice_fusion.12
  145.4 17.4 %copy.126 = f32[24,512,16,24]{1,3,2,0:T(8,128)S(1)} copy(f32[24,512,16,24]{1,2,3,0:T(8,128)} %subtract_dynamic-update-slice_fusion) | data formatting | bytes 37748736 | tf_op jit(solution)/shard_map/stack | solution.py:77
  162.9 6.6 %fusion.20 = bf16[24,512,384]{1,2,0:T(8,128)(2,1)} fusion(f32[24,512,16,24]{1,3,2,0:T(8,128)S(1)} %copy.126, f32[24]{0:T(128)S(1)} %copy-done.40, f32[512]{0:T(512)S(1)} %fusion.337, f32[24,384]{1,0:T(8,128)S(1)} %fusion.38), kind=kLoop, calls=%fused_computation.30 | loop fusion | flops 18874368 | bytes 28350560 | tf_op jit(solution)/shard_map/convert_element_type | solution.py:87
  169.5 7.9 %reshape.8825 = bf16[768,32,32]{2,1,0:T(8,128)(2,1)} reshape(bf16[16,2,24576]{2,1,0:T(2,128)(2,1)} %all-to-all-done) | data formatting | bytes 3145728
  177.4 9.4 %copy.129 = bf16[16,48,32,32]{2,0,3,1:T(8,128)(2,1)} copy(bf16[16,48,32,32]{3,2,1,0:T(8,128)(2,1)} %bitcast.86) | data formatting | bytes 3145728 | tf_op jit(solution)/shard_map/all_to_all | solution.py:121
  186.8 9.4 %reshape.8814 = bf16[24,2,512,32]{2,3,1,0:T(8,128)(2,1)} reshape(bf16[48,16,32,32]{2,1,3,0:T(8,128)(2,1)} %bitcast.87) | data formatting | bytes 3145728 | tf_op jit(solution)/shard_map/reshape | solution.py:128
  196.2 7.0 %fusion.352 = f32[24,384,64]{1,2,0:S(1)} fusion(bf16[24,512,384]{1,2,0:T(8,128)(2,1)} %fusion.20, bf16[24,512,64]{1,2,0:T(8,128)(2,1)} %bitcast.90), kind=kOutput, calls=%fused_computation.517 | convolution fusion | flops 603979776 | bytes 13369344
  203.5 2.0 copy.131
  205.4 4.5 %all_to_all.28 = bf16[32,2,9216]{2,1,0:T(2,128)(2,1)} reshape(bf16[32,24,2,384]{3,2,1,0:T(2,128)(2,1)} %copy.131) | data formatting | bytes 2359296 | tf_op jit(solution)/shard_map/all_to_all | solution.py:135
  211.4 18.3 %all_to_all.34 = bf16[32,2,9216]{2,0,1:T(8,128)(2,1)S(1)} all-to-all(bf16[32,2,9216]{2,0,1:T(8,128)(2,1)S(1)} %copy.132), channel_id=1, replica_groups=mesh['lat'=16,'tm'=2] {'tm'}, dimensions={1} | all-to-all | bytes 2359296 | tf_op jit(solution)/shard_map/all_to_all | solution.py:135
  230.8 10.2 %reduce-scatter.2.cloned.1.call-done = f32[32,64]{1,0:T(8,128)} async-done(((f32[64,64]{1,0:T(8,128)}), f32[32,64]{1,0:T(8,128)}) %reduce-scatter.2.cloned.1.call-update) | async-done | bytes 8208 | tf_op jit(solution)/shard_map/reduce_scatter | solution.py:136
  241.0 22.3 %all-gather = f32[512,64]{1,0:T(8,128)S(1)} all-gather(f32[32,64]{1,0:T(8,128)} %reduce-scatter.2.cloned.1.call-done), channel_id=2, replica_groups=mesh['lat'=16,'tm'=2] {'lat'}, dimensions={0}, use_global_device_ids=true | all-gather | bytes 139264 | tf_op jit(solution)/shard_map/all_gather | solution.py:144
  264.7 5.5 %psum.7 = f32[]{:T(128)} all-reduce(f32[]{:T(128)} %reduce_sum.19), channel_id=1, replica_groups=mesh['lat'=16,'tm'=2] {'tm'}, use_global_device_ids=true, to_apply=%region_5.6 | all-reduce | flops 1 | bytes 8 | tf_op jit(solution)/shard_map/psum | solution.py:146
  (373 shorter events, 82.1 us)
Async XLA Ops:
  44.8 124.8 %all-to-all-start = ((bf16[16,2,24576]{2,1,0:T(2,128)(2,1)}), bf16[16,2,24576]{2,1,0:T(2,128)(2,1)}, u32[]{:S(2)}, u32[]{:S(2)}) async-start(bf16[16,2,24576]{2,1,0:T(2,128)(2,1)} %reshape.8824), calls=%async_computation | async-start | bytes 3145728 | tf_op jit(solution)/shard_map/all_to_all | solution.py:121
  52.2 188.8 %reduce-scatter.2.cloned.1.call-start = ((), (), s32[]{:S(2)}) async-start(), calls=%async_computation.3 | async-start | bytes 49152 | tf_op jit(solution)/shard_map/reduce_scatter | solution.py:136
  52.5 34.0 %copy-start.38 = (f32[24]{0:T(128)}, f32[24]{0:T(128)S(1)}, u32[]{:S(2)}) copy-start(f32[24]{0:T(128)S(1)} %add_convert_fusion) | copy-start | bytes 292
  87.4 29.3 %copy-start.6 = (f32[24,16]{1,0:T(8,128)}, f32[24,16]{1,0:T(8,128)S(1)}, u32[]{:S(2)}) copy-start(f32[24,16]{1,0:T(8,128)S(1)} %copy.79) | copy-start | bytes 4612
  87.4 29.2 %copy-start.7 = (f32[24,16]{1,0:T(8,128)}, f32[24,16]{1,0:T(8,128)S(1)}, u32[]{:S(2)}) copy-start(f32[24,16]{1,0:T(8,128)S(1)} %copy.80) | copy-start | bytes 4612
  87.5 29.1 %copy-start.16 = (f32[24,16]{1,0:T(8,128)}, f32[24,16]{1,0:T(8,128)S(1)}, u32[]{:S(2)}) copy-start(f32[24,16]{1,0:T(8,128)S(1)} %copy.81) | copy-start | bytes 4612
  87.6 29.0 %copy-start.17 = (f32[24,16]{1,0:T(8,128)}, f32[24,16]{1,0:T(8,128)S(1)}, u32[]{:S(2)}) copy-start(f32[24,16]{1,0:T(8,128)S(1)} %copy.82) | copy-start | bytes 4612
  109.7 17.6 %copy-start.12 = (f32[24,16]{1,0:T(8,128)S(1)}, f32[24,16]{1,0:T(8,128)}, u32[]{:S(2)}) copy-start(f32[24,16]{1,0:T(8,128)} %copy.97) | copy-start | bytes 4612
  109.7 17.6 %copy-start.13 = (f32[24,16]{1,0:T(8,128)S(1)}, f32[24,16]{1,0:T(8,128)}, u32[]{:S(2)}) copy-start(f32[24,16]{1,0:T(8,128)} %copy.98) | copy-start | bytes 4612
  109.7 18.8 %copy-start.28 = (f32[24,16]{1,0:T(8,128)S(1)}, f32[24,16]{1,0:T(8,128)}, u32[]{:S(2)}) copy-start(f32[24,16]{1,0:T(8,128)} %copy.100) | copy-start | bytes 4612
  109.7 18.8 %copy-start.30 = (f32[24,16]{1,0:T(8,128)S(1)}, f32[24,16]{1,0:T(8,128)}, u32[]{:S(2)}) copy-start(f32[24,16]{1,0:T(8,128)} %copy.99) | copy-start | bytes 4612
  109.7 20.1 %copy-start.25 = (f32[24,16]{1,0:T(8,128)S(1)}, f32[24,16]{1,0:T(8,128)}, u32[]{:S(2)}) copy-start(f32[24,16]{1,0:T(8,128)} %copy.101) | copy-start | bytes 4612
  109.7 20.1 %copy-start.27 = (f32[24,16]{1,0:T(8,128)S(1)}, f32[24,16]{1,0:T(8,128)}, u32[]{:S(2)}) copy-start(f32[24,16]{1,0:T(8,128)} %copy.102) | copy-start | bytes 4612
  112.9 19.4 %copy-start.10 = (f32[24,16]{1,0:T(8,128)S(1)}, f32[24,16]{1,0:T(8,128)}, u32[]{:S(2)}) copy-start(f32[24,16]{1,0:T(8,128)} %copy.105) | copy-start | bytes 4612
  113.0 19.4 %copy-start.11 = (f32[24,16]{1,0:T(8,128)S(1)}, f32[24,16]{1,0:T(8,128)}, u32[]{:S(2)}) copy-start(f32[24,16]{1,0:T(8,128)} %copy.106) | copy-start | bytes 4612
  114.1 19.5 %copy-start.24 = (f32[24,16]{1,0:T(8,128)S(1)}, f32[24,16]{1,0:T(8,128)}, u32[]{:S(2)}) copy-start(f32[24,16]{1,0:T(8,128)} %copy.107) | copy-start | bytes 4612
  114.1 19.5 %copy-start.26 = (f32[24,16]{1,0:T(8,128)S(1)}, f32[24,16]{1,0:T(8,128)}, u32[]{:S(2)}) copy-start(f32[24,16]{1,0:T(8,128)} %copy.108) | copy-start | bytes 4612
  115.3 19.6 %copy-start.22 = (f32[24,16]{1,0:T(8,128)S(1)}, f32[24,16]{1,0:T(8,128)}, u32[]{:S(2)}) copy-start(f32[24,16]{1,0:T(8,128)} %copy.109) | copy-start | bytes 4612
  115.3 19.6 %copy-start.23 = (f32[24,16]{1,0:T(8,128)S(1)}, f32[24,16]{1,0:T(8,128)}, u32[]{:S(2)}) copy-start(f32[24,16]{1,0:T(8,128)} %copy.110) | copy-start | bytes 4612
  118.8 17.5 %copy-start.9 = (f32[24,16]{1,0:T(8,128)S(1)}, f32[24,16]{1,0:T(8,128)}, u32[]{:S(2)}) copy-start(f32[24,16]{1,0:T(8,128)} %copy.112) | copy-start | bytes 4612
  118.8 18.6 %copy-start.20 = (f32[24,16]{1,0:T(8,128)S(1)}, f32[24,16]{1,0:T(8,128)}, u32[]{:S(2)}) copy-start(f32[24,16]{1,0:T(8,128)} %copy.113) | copy-start | bytes 4612
  118.8 18.6 %copy-start.21 = (f32[24,16]{1,0:T(8,128)S(1)}, f32[24,16]{1,0:T(8,128)}, u32[]{:S(2)}) copy-start(f32[24,16]{1,0:T(8,128)} %copy.114) | copy-start | bytes 4612
  145.4 17.5 %copy-start.40 = (f32[24]{0:T(128)S(1)}, f32[24]{0:T(128)}, u32[]{:S(2)}) copy-start(f32[24]{0:T(128)} %get-tuple-element.429) | copy-start | bytes 292
  186.8 84.7 %copy-start.1 = (bf16[32,32,1024]{2,1,0:T(8,128)(2,1)S(1)}, bf16[32,32,1024]{2,1,0:T(8,128)(2,1)}, u32[]{:S(2)}) copy-start(bf16[32,32,1024]{2,1,0:T(8,128)(2,1)} %param.3) | copy-start | bytes 6291460
  (19 other events, 266.9 us)
Sparse Core Ops, SparseCore 0:
  230.9 10.0 reduce-scatter.1
